TPU v7x, 32 devices: a whole 2x2x4 slice. The times are simulated.
32 devices in a mesh: feat: 8 (over y, x, core), rep: 4 (over z).
Axes of the slice: x: 2, y: 2, z: 4, core: 2. Of those that a mesh axis runs over, the one named last changes fastest.
Arguments:
- features: bfloat16 [4, 8, 1024, 512], P('rep', None, 'feat'), may hold values from -6 to 6
- adjacency_one: int32 [4, 8, 5, 16, 512], P('rep'), may hold values from 0 to 65535, as said below
- pre_hidden: bfloat16 [4, 8, 256, 256], P('rep', 'feat'), may hold values from -6 to 6
- adjacency_two: int32 [4, 8, 5, 8, 256], P('rep', 'feat'), may hold values from 0 to 65535, as said below
- weight_two: bfloat16 [6, 256, 256], replicated, may hold values from -0.375 to 0.375
- out_grad: bfloat16 [4, 8, 128, 256], P('rep', 'feat'), may hold values from -6 to 6
Outputs:
- grad_w1: float32 [6, 1024, 256], P(None, 'feat')
- grad_b1: float32 [256], replicated
- grad_w2: float32 [6, 256, 256], replicated
- grad_b2: float32 [256], replicated
Inputs may be any that keep to these rules, and one draw needn't show every extreme that they name: `adjacency_one`: bit k, k below 16, of word (w, n) is the entry of destination row 16 w + k and source column n; higher bits are zero; some rows are empty. `adjacency_two`: bit k, k below 16, of word (w, n) is the entry of seed row 16 w + k and source column n; higher bits are zero; some rows are empty.
All inputs are finite; a program needn't handle non-finite values.
Results may differ from a plain program's by a relative error of at most 0.0041.
Values may be sent and summed in bfloat16 or wider, within the bound.
No kernel may reach another device: no remote copies, remote signals or barrier semaphores. Data moves between devices by JAX's collectives and lax.ppermute only.
A program may use at most 128 MiB of HBM per device.

v0:
```python
import math
import jax
import jax.numpy as jnp
from jax import lax
from jax.sharding import PartitionSpec as P


def unpack(packed):
    shifts = jnp.arange(16, dtype=jnp.int32)
    spread = jnp.bitwise_and(jnp.right_shift(packed[..., None, :], shifts[:, None]), 1)
    dense = spread.reshape(packed.shape[:-2] + (packed.shape[-2] * 16, packed.shape[-1]))
    degree = jnp.sum(dense, axis=-1).astype(jnp.float32)
    return (dense.astype(jnp.bfloat16), 1.0 / jnp.maximum(degree, 1.0))


def upper_layer(pre_rows, words_two, grad_rows, weight_two, factor):
    hidden = jnp.maximum(pre_rows, 0)
    seed_count = grad_rows.shape[0]
    matrix, inverse = unpack(words_two)
    mixed = (
        jnp.einsum("rsd,dh->rsh", matrix, hidden, preferred_element_type=jnp.float32)
        * inverse[..., None]
    ).astype(jnp.bfloat16)
    scaled = grad_rows.astype(jnp.float32) * factor
    scaled_low = scaled.astype(jnp.bfloat16)
    grad_rel = jnp.einsum("rsh,sk->rhk", mixed, scaled_low, preferred_element_type=jnp.float32)
    grad_self = jnp.einsum(
        "sh,sk->hk", hidden[:seed_count], scaled_low, preferred_element_type=jnp.float32
    )
    weight_grad = jnp.concatenate([grad_self[None], grad_rel], 0)
    backed = (
        jnp.einsum("sk,rhk->rsh", scaled_low, weight_two[1:], preferred_element_type=jnp.float32)
        * inverse[..., None]
    ).astype(jnp.bfloat16)
    spread_back = jnp.einsum("rsd,rsh->dh", matrix, backed, preferred_element_type=jnp.float32)
    own_part = jnp.einsum(
        "sk,hk->sh", scaled_low, weight_two[0], preferred_element_type=jnp.float32
    )
    hidden_total = spread_back + jnp.pad(own_part, ((0, hidden.shape[0] - seed_count), (0, 0)))
    hidden_grad = jnp.where(pre_rows > 0, hidden_total, 0.0).astype(jnp.bfloat16)
    return (
        weight_grad,
        jnp.sum(scaled, 0),
        hidden_grad,
        jnp.sum(hidden_grad.astype(jnp.float32), 0),
    )


def panel_terms(word_block, column_block, grad_block):
    matrix, inverse = unpack(word_block)
    rows_one = grad_block.shape[1]
    gathered = (
        jnp.einsum("brdn,bcn->brdc", matrix, column_block, preferred_element_type=jnp.float32)
        * inverse[..., None]
    ).astype(jnp.bfloat16)
    panel_rel = jnp.einsum(
        "brdc,bdh->rch", gathered, grad_block, preferred_element_type=jnp.float32
    )
    panel_self = jnp.einsum(
        "bcd,bdh->ch", column_block[:, :, :rows_one], grad_block, preferred_element_type=jnp.float32
    )
    return jnp.concatenate([panel_self[None], panel_rel], 0)


def on_device(features, adjacency_one, pre_hidden, adjacency_two, weight_two, out_grad):
    seed_count = out_grad.shape[2]
    factor = float(seed_count * lax.axis_size("feat") * lax.axis_size("rep")) ** (-0.5)
    weight_grad, bias_two, hidden_grad, bias_one = upper_layer(
        pre_hidden[0, 0], adjacency_two[0, 0], out_grad[0, 0], weight_two, factor
    )
    feature_local = features[0]
    adj_local = adjacency_one[0]
    col_width = feature_local.shape[1]
    hidden_width = hidden_grad.shape[1]
    relations = adj_local.shape[1]
    initial = jnp.zeros((relations + 1, col_width, hidden_width), jnp.float32)
    piece = lax.all_gather(hidden_grad[None], "feat", axis=0, tiled=True)
    piece_rows = piece.shape[0]
    group_size = math.gcd(piece_rows, 8)
    turn_count = piece_rows // group_size
    word_block = adj_local
    word_block = word_block.reshape((turn_count, group_size) + adj_local.shape[1:])
    column_block = feature_local
    column_block = column_block.reshape((turn_count, group_size) + feature_local.shape[1:])
    grad_block = piece.reshape((turn_count, group_size) + piece.shape[1:])

    def one_turn(running, inputs):
        return (running + panel_terms(inputs[0], inputs[1], inputs[2]), None)

    running, unused = lax.scan(one_turn, initial, (word_block, column_block, grad_block))
    grad_w1 = lax.psum(running, "rep")
    grad_w2, grad_b1, grad_b2 = lax.psum((weight_grad, bias_one, bias_two), ("feat", "rep"))
    return (grad_w1, grad_b1, grad_w2, grad_b2)


def solution(mesh):
    placed = (
        P("rep", None, "feat", None),
        P("rep", None, None, None, None),
        P("rep", "feat", None, None),
        P("rep", "feat", None, None, None),
        P(),
        P("rep", "feat", None, None),
    )
    return jax.shard_map(
        on_device,
        mesh=mesh,
        in_specs=placed,
        out_specs=(P(None, "feat", None), P(), P(), P()),
        check_vma=False,
    )
```

profile of v0, /device:TPU:0, one launch (start us, length us, event | category | flops | bytes accessed | tf_op | source)
XLA Modules:
  0.0 213.1 jit_solution(5158156742498113044)
XLA Ops:
  8.0 0.0 copy-start
  8.0 0.0 all-gather.3.cloned.1.call-start
  8.1 1.6 fusion.28
  9.7 0.1 div.22
  9.8 0.1 shift_right_arithmetic.72
  9.9 0.9 fusion.27
  10.8 1.1 fusion.37
  11.9 2.4 %convert_reduce_fusion = (f32[256]{0:T(256)S(1)}, bf16[256,256]{1,0:T(8,128)(2,1)}) fusion(f32[128,256]{1,0:T(8,128)S(1)} %fusion.37, bf16[5,128,256]{2,1,0:T(8,128)(2,1)S(1)} %fusion.27, bf16[6,256,256]{2,1,0:T(8,128)(2,1)} %param.10, f32[5,128]{1,0:T(8,128)S(1)} %div.22, bf16[1,1,128,256]{3,2,1,0:T(8,128)(2,1)} %param.11, bf16[1,1,256,256]{3,2,1,0:T(8,128)(2,1)} %param.8), kind=kOutput, calls=%fused_computation.38 | convolution fusion | flops 168722176 | bytes 1445376 | tf_op jit(solution)/shard_map/rsd,rsh->dh/dot_general | solution.py:35
  14.4 0.0 all-gather.3.cloned.1.call-update
  14.4 0.0 all-reduce.7.cloned.1.call-start
  14.4 0.9 broadcast_maximum_fusion
  15.4 1.0 convolution_bitcast_fusion.1
  16.4 1.6 fusion.19
  18.0 1.2 pad_maximum_fusion
  19.3 0.0 all-reduce.7.cloned.1.call-update
  19.3 0.2 all-reduce.5.cloned.1.call-start
  19.5 0.0 copy-done
  19.5 10.9 %and_reduce_fusion = s32[8,5,16,16]{3,2,1,0:T(8,128)S(1)} fusion(s32[8,5,16,512]{3,2,1,0:T(8,128)S(1)} %bitcast.90), kind=kLoop, calls=%fused_computation.3 | loop fusion | flops 15718400 | bytes 1351680 | tf_op jit(solution)/shard_map/while/body/eval_jaxpr/reduce_sum | solution.py:12
  30.4 0.1 maximum_divide_fusion
  30.5 0.2 reshape.90
  30.7 0.1 shift_right_arithmetic.81
  30.7 10.1 %all-gather.3.cloned.1.call-done = bf16[2048,256]{1,0:T(8,128)(2,1)} async-done(((bf16[256,256]{1,0:T(8,128)(2,1)}), bf16[2048,256]{1,0:T(8,128)(2,1)}) %all-gather.3.cloned.1.call-update) | async-done | bytes 1048592 | tf_op jit(solution)/shard_map/all_gather | solution.py:77
  40.9 0.0 copy-start.2
  40.9 0.0 copy-start.3
  40.9 10.5 %shift_right_arithmetic.78 = s32[8,5,16,16,512]{4,3,2,1,0:T(8,128)} broadcast(s32[8,5,16,512]{3,2,1,0:T(8,128)S(1)} %bitcast.91), dimensions={0,1,2,4} | broadcast | bytes 22282240 | tf_op jit(solution)/shard_map/while/body/eval_jaxpr/shift_right_arithmetic | solution.py:10
  51.3 0.0 copy-done.2
  51.3 0.0 copy-done.3
  51.3 0.0 copy-start.1
  51.3 9.5 %fusion.13 = f32[5,128,256]{2,1,0:T(8,128)S(1)} fusion(bf16[8,256,256,1]{2,1,0,3:T(8,128)(2,1)S(1)} %bitcast.96, f32[8,5,256]{2,0,1:T(8,128)S(1)} %copy.37, s32[8,5,256,512]{3,2,1,0:T(8,128)} %bitcast.89, s32[256]{0:T(256)S(1)} %shift_right_arithmetic.81, bf16[1,8,128,512]{3,2,1,0:T(8,128)(2,1)S(1)} %copy-done.2), kind=kOutput, calls=%fused_computation.14 | convolution fusion | flops 2031616000 | bytes 23766016 | tf_op jit(solution)/shard_map/while/body/eval_jaxpr/brdc,bdh->rch/dot_general | solution.py:56
  60.8 0.5 convolution_bitcast_fusion.2
  61.3 0.1 copy.30
  61.4 1.0 pad_maximum_fusion.1
  62.4 0.0 all-reduce.5.cloned.1.call-update
  62.4 0.0 copy-done.1
  62.4 39.3 %all-reduce.1 = (f32[256]{0:T(256)}, f32[256]{0:T(256)}) all-reduce(f32[256]{0:T(256)S(1)} %get-tuple-element.23, f32[256]{0:T(256)S(1)} %fusion.40), channel_id=1, replica_groups=mesh['feat'=8,'rep'=4] {'feat','rep'}, use_global_device_ids=true, to_apply=%region_4.5 | all-reduce | flops 512 | bytes 4096 | tf_op jit(solution)/shard_map/psum | solution.py:92
  101.8 53.7 %all-reduce.7.cloned.1.call-done = f32[6,256,256]{2,1,0:T(8,128)} async-done(((f32[6,256,256]{2,1,0:T(8,128)}), f32[6,256,256]{2,1,0:T(8,128)}) %all-reduce.7.cloned.1.call-update) | async-done | bytes 1572880 | tf_op jit(solution)/shard_map/psum | solution.py:92
  155.4 45.4 %all-reduce.5.cloned.1.call-done = f32[6,128,256]{2,1,0:T(8,128)} async-done(((f32[6,128,256]{2,1,0:T(8,128)}), f32[6,128,256]{2,1,0:T(8,128)}) %all-reduce.5.cloned.1.call-update) | async-done | bytes 786448 | tf_op jit(solution)/shard_map/psum | solution.py:91
  200.8 2.1 copy.52
  202.9 2.7 %copy.53 = f32[6,256,256]{2,1,0:T(8,128)} copy(f32[6,256,256]{2,1,0:T(8,128)} %all-reduce.7.cloned.1.call-done) | data formatting | bytes 3145728
  (5 shorter events, 0.1 us)
Async XLA Ops:
  8.0 11.5 %copy-start = (s32[1,8,5,16,512]{4,3,2,1,0:T(8,128)S(1)}, s32[1,8,5,16,512]{4,3,2,1,0:T(8,128)}, u32[]{:S(2)}) copy-start(s32[1,8,5,16,512]{4,3,2,1,0:T(8,128)} %param.7) | copy-start | bytes 3932164
  8.0 32.9 %all-gather.3.cloned.1.call-start = ((), (), s32[]{:S(2)}) async-start(), calls=%async_computation.2 | async-start | bytes 1179648 | tf_op jit(solution)/shard_map/all_gather | solution.py:77
  14.4 141.0 %all-reduce.7.cloned.1.call-start = ((), (), s32[]{:S(2)}) async-start(), calls=%async_computation.1 | async-start | bytes 3145728 | tf_op jit(solution)/shard_map/psum | solution.py:92
  19.3 181.5 %all-reduce.5.cloned.1.call-start = ((), (), s32[]{:S(2)}) async-start(), calls=%async_computation | async-start | bytes 1572864 | tf_op jit(solution)/shard_map/psum | solution.py:91
  40.9 10.5 %copy-start.2 = (bf16[1,8,128,512]{3,2,1,0:T(8,128)(2,1)S(1)}, bf16[1,8,128,512]{3,2,1,0:T(8,128)(2,1)}, u32[]{:S(2)}) copy-start(bf16[1,8,128,512]{3,2,1,0:T(8,128)(2,1)} %param.6) | copy-start | bytes 3145732
  40.9 10.5 %copy-start.3 = (bf16[2048,256]{1,0:T(8,128)(2,1)S(1)}, bf16[2048,256]{1,0:T(8,128)(2,1)}, u32[]{:S(2)}) copy-start(bf16[2048,256]{1,0:T(8,128)(2,1)} %all-gather.3.cloned.1.call-done) | copy-start | bytes 3145732
  51.3 11.0 %copy-start.1 = (bf16[1,1,128,256]{3,2,1,0:T(8,128)(2,1)S(1)}, bf16[1,1,128,256]{3,2,1,0:T(8,128)(2,1)}, u32[]{:S(2)}) copy-start(bf16[1,1,128,256]{3,2,1,0:T(8,128)(2,1)} %param.11) | copy-start | bytes 196612
Sparse Core Ops, SparseCore 0:
  14.5 26.3 all-gather.2
Sparse Core Ops, SparseCore 1:
  20.7 134.6 all-reduce.6
  158.2 42.5 all-reduce.4
where the time goes:
time: 214 us; the launch traced here: 213 us
  waiting for transfers between devices  109 us (51%)
  blocking collectives  39.3 us (18%)
  other arithmetic  16.6 us (8%)
  matrix products  16.1 us (8%)
  local copies, waits for them, and re-layouts  15.8 us (7%)
  between operations  15.6 us (7%)
    psum x1, waiting for transfers between devices, on_device(): lax.psum((weight_grad, bias_one, bias_two), ('feat', 'rep'))  53.7 us
    psum x1, waiting for transfers between devices, on_device(): grad_w1 = lax.psum(running, 'rep')  45.4 us
    psum x1, blocking collectives, on_device(): lax.psum((weight_grad, bias_one, bias_two), ('feat', 'rep'))  39.3 us
    reduce_sum x1, other arithmetic, unpack(): degree = jnp.sum(dense, axis=-1).astype(jnp.float32)  10.9 us
    shift_right_arithmetic x5, local copies, waits for them, and re-layouts, unpack(): jnp.right_shift(packed[..., None, :], shifts[:, None])  10.6 us
    all_gather x1, waiting for transfers between devices, on_device(): piece = lax.all_gather(hidden_grad[None], 'feat', axis=0, tiled=True)  10.1 us
    dot_general x1, matrix products, panel_terms(): jnp.einsum('brdc,bdh->rch', gathered, grad_block, preferred_element_type=...  9.46 us
    unnamed x10, local copies, waits for them, and re-layouts  4.85 us
  transfers between devices with their start and end apart: 3, of which 3 were waited for; matrix products, arithmetic and copies ran while one was open for 18% of the time, Pallas kernels for 0%

commit v1 on v0

--- a/solution.py
+++ b/solution.py
@@ -88,7 +88,7 @@
         return (running + panel_terms(inputs[0], inputs[1], inputs[2]), None)
 
     running, unused = lax.scan(one_turn, initial, (word_block, column_block, grad_block))
-    grad_w1 = lax.psum(running, "rep")
+    grad_w1 = jnp.sum(lax.all_gather(running, "rep"), axis=0)
     grad_w2, grad_b1, grad_b2 = lax.psum((weight_grad, bias_one, bias_two), ("feat", "rep"))
     return (grad_w1, grad_b1, grad_w2, grad_b2)
 

time: 214 us -> 244 us (1.14)
  waiting for transfers between devices: 109 us -> 141 us
  local copies, waits for them, and re-layouts: 15.8 us -> 3.27 us
  other arithmetic: 16.6 us -> 26.3 us
  blocking collectives: 39.3 us -> 44 us
  matrix products: 16.1 us -> 13.2 us
    psum x1, waiting for transfers between devices: 53.7 us -> 113 us  [on_device(): lax.psum((weight_grad, bias_one, bias_two), ('feat', 'rep'))]
    psum x1 -> x0, waiting for transfers between devices: 45.4 us -> none  [on_device(): grad_w1 = lax.psum(running, 'rep')]
    all_gather x0 -> x1, waiting for transfers between devices: none -> 20.6 us  [on_device(): grad_w1 = jnp.sum(lax.all_gather(running, 'rep'), axis=0)]
    shift_right_arithmetic x5 -> x4, local copies, waits for them, and re-layouts: 10.6 us -> 0.17 us  [unpack(): jnp.right_shift(packed[..., None, :], shifts[:, None])]
    convert_element_type x2 -> x3, other arithmetic: 2.55 us -> 9.85 us  [unpack(): return (dense.astype(jnp.bfloat16), 1.0 / jnp.maximum(degree, 1.0))]
    psum x1, blocking collectives: 39.3 us -> 44 us  [on_device(): lax.psum((weight_grad, bias_one, bias_two), ('feat', 'rep'))]
    reduce_sum x0 -> x1, other arithmetic: none -> 3.07 us  [on_device(): grad_w1 = jnp.sum(lax.all_gather(running, 'rep'), axis=0)]
    all_gather x1, waiting for transfers between devices: 10.1 us -> 7.53 us  [on_device(): piece = lax.all_gather(hidden_grad[None], 'feat', axis=0, tiled=True)]
  transfers between devices with their start and end apart: 3 -> 3, of which waited for: 3 -> 3; matrix products, arithmetic and copies ran while one was open for 18% -> 10% of each run, Pallas kernels for 0% -> 0%
where the time goes in v1:
time: 244 us
  waiting for transfers between devices  141 us (58%)
  blocking collectives  44 us (18%)
  other arithmetic  26.3 us (11%)
  between operations  15.6 us (6%)
  matrix products  13.2 us (5%)
  local copies, waits for them, and re-layouts  3.27 us (1%)
    psum x1, waiting for transfers between devices, on_device(): lax.psum((weight_grad, bias_one, bias_two), ('feat', 'rep'))  113 us
    psum x1, blocking collectives, on_device(): lax.psum((weight_grad, bias_one, bias_two), ('feat', 'rep'))  44 us
    all_gather x1, waiting for transfers between devices, on_device(): grad_w1 = jnp.sum(lax.all_gather(running, 'rep'), axis=0)  20.6 us
    reduce_sum x1, other arithmetic, unpack(): degree = jnp.sum(dense, axis=-1).astype(jnp.float32)  11 us
    convert_element_type x3, other arithmetic, unpack(): return (dense.astype(jnp.bfloat16), 1.0 / jnp.maximum(degree, 1.0))  9.85 us
    all_gather x1, waiting for transfers between devices, on_device(): piece = lax.all_gather(hidden_grad[None], 'feat', axis=0, tiled=True)  7.53 us
    dot_general x1, matrix products, panel_terms(): jnp.einsum('brdc,bdh->rch', gathered, grad_block, preferred_element_type=...  7.01 us
  transfers between devices with their start and end apart: 3, of which 3 were waited for; matrix products, arithmetic and copies ran while one was open for 10% of the time, Pallas kernels for 0%

profile of v1, /device:TPU:0, one launch (start us, length us, event | category | flops | bytes accessed | tf_op | source)
XLA Modules:
  0.0 243.7 jit_solution(4107933674266037306)
XLA Ops:
  8.0 0.0 copy-start
  8.0 0.0 all-gather.5.cloned.1.call-start
  8.1 1.6 fusion.20
  9.7 0.1 div.22
  9.8 0.1 shift_right_arithmetic.72
  9.9 0.9 fusion.19
  10.8 1.1 fusion.29
  11.9 2.4 convert_reduce_fusion
  14.4 0.0 all-gather.5.cloned.1.call-update
  14.4 0.0 all-gather.7.cloned.1.call-start
  14.5 0.1 shift_right_arithmetic.81
  14.5 0.0 copy-done
  14.5 7.3 %fusion.1 = bf16[8,5,256,512]{3,2,0,1:T(8,128)(2,1)} fusion(s32[256]{0:T(256)S(1)} %shift_right_arithmetic.81, s32[1,8,5,16,512]{4,3,2,1,0:T(8,128)S(1)} %copy-done), kind=kLoop, calls=%fused_computation.2 | loop fusion | flops 15728640 | bytes 11797504 | tf_op jit(solution)/shard_map/while/body/eval_jaxpr/convert_element_type | solution.py:13
  21.8 0.0 copy-start.3
  21.8 11.0 %and_reduce_fusion = s32[8,5,16,16]{3,2,0,1:T(8,128)S(1)} fusion(s32[1,8,5,16,512]{4,3,2,1,0:T(8,128)S(1)} %copy-done), kind=kLoop, calls=%fused_computation.3 | loop fusion | flops 15718400 | bytes 1351680 | tf_op jit(solution)/shard_map/while/body/eval_jaxpr/reduce_sum | solution.py:12
  32.9 0.1 maximum_divide_fusion
  32.9 0.2 div.24
  33.1 7.5 %all-gather.5.cloned.1.call-done = bf16[2048,256]{1,0:T(8,128)(2,1)} async-done(((bf16[256,256]{1,0:T(8,128)(2,1)}), bf16[2048,256]{1,0:T(8,128)(2,1)}) %all-gather.5.cloned.1.call-update) | async-done | bytes 1048592 | tf_op jit(solution)/shard_map/all_gather | solution.py:77
  40.7 0.0 copy-done.3
  40.7 1.7 convolution_bitcast_fusion.2
  42.4 0.1 copy.22
  42.5 0.0 copy-start.2
  42.5 7.0 %fusion.6 = f32[5,128,256]{2,1,0:T(8,128)S(1)} fusion(bf16[8,256,256,1]{2,1,0,3:T(8,128)(2,1)} %bitcast.110, f32[8,5,256]{2,0,1:T(8,128)S(1)} %div.24, bf16[8,5,256,512]{3,2,0,1:T(8,128)(2,1)} %fusion.1, bf16[1,8,128,512]{3,2,1,0:T(8,128)(2,1)} %param.6), kind=kOutput, calls=%fused_computation.9 | convolution fusion | flops 2015887360 | bytes 13279232 | tf_op jit(solution)/shard_map/while/body/eval_jaxpr/brdc,bdh->rch/dot_general | solution.py:56
  49.5 0.0 copy-start.1
  49.5 0.9 pad_maximum_fusion.1
  50.4 0.0 all-gather.7.cloned.1.call-update
  50.5 0.0 all-reduce.4.cloned.1.call-start
  50.5 0.0 copy-done.2
  50.5 0.0 copy-done.1
  50.5 0.2 convolution_bitcast_fusion.1
  50.8 0.7 fusion.11
  51.5 1.2 pad_maximum_fusion
  52.7 0.0 all-reduce.4.cloned.1.call-update
  52.8 44.0 %all-reduce.1 = (f32[256]{0:T(256)}, f32[256]{0:T(256)}) all-reduce(f32[256]{0:T(256)S(1)} %get-tuple-element.23, f32[256]{0:T(256)S(1)} %fusion.32), channel_id=1, replica_groups=mesh['feat'=8,'rep'=4] {'feat','rep'}, use_global_device_ids=true, to_apply=%region_4.5 | all-reduce | flops 512 | bytes 4096 | tf_op jit(solution)/shard_map/psum | solution.py:92
  96.7 20.6 %all-gather.7.cloned.1.call-done = f32[24,128,256]{2,1,0:T(8,128)} async-done(((f32[6,128,256]{2,1,0:T(8,128)}), f32[24,128,256]{2,1,0:T(8,128)}) %all-gather.7.cloned.1.call-update) | async-done | bytes 3145744 | tf_op jit(solution)/shard_map/all_gather | solution.py:91
  117.3 3.1 %reduce_sum.48 = f32[6,128,256]{2,1,0:T(8,128)} reduce(f32[4,6,128,256]{3,2,1,0:T(8,128)} %bitcast.104, f32[]{:T(128)} %constant.13.clone.1), dimensions={0}, to_apply=%region_2.3 | reduce | flops 589824 | bytes 3932164 | tf_op jit(solution)/shard_map/reduce_sum | solution.py:91
  120.4 113.2 %all-reduce.4.cloned.1.call-done = f32[6,256,256]{2,1,0:T(8,128)} async-done(((f32[6,256,256]{2,1,0:T(8,128)}), f32[6,256,256]{2,1,0:T(8,128)}) %all-reduce.4.cloned.1.call-update) | async-done | bytes 1572880 | tf_op jit(solution)/shard_map/psum | solution.py:92
  233.5 2.7 %copy.34 = f32[6,256,256]{2,1,0:T(8,128)} copy(f32[6,256,256]{2,1,0:T(8,128)} %all-reduce.4.cloned.1.call-done) | data formatting | bytes 3145728
  (5 shorter events, 0.1 us)
Async XLA Ops:
  8.0 6.5 %copy-start = (s32[1,8,5,16,512]{4,3,2,1,0:T(8,128)S(1)}, s32[1,8,5,16,512]{4,3,2,1,0:T(8,128)}, u32[]{:S(2)}) copy-start(s32[1,8,5,16,512]{4,3,2,1,0:T(8,128)} %param.7) | copy-start | bytes 3932164
  8.0 32.6 %all-gather.5.cloned.1.call-start = ((), (), s32[]{:S(2)}) async-start(), calls=%async_computation.1 | async-start | bytes 1179648 | tf_op jit(solution)/shard_map/all_gather | solution.py:77
  14.4 102.9 %all-gather.7.cloned.1.call-start = ((), (), s32[]{:S(2)}) async-start(), calls=%async_computation.2 | async-start | bytes 3932160 | tf_op jit(solution)/shard_map/all_gather | solution.py:91
  21.8 18.8 %copy-start.3 = (bf16[1,8,128,512]{3,2,1,0:T(8,128)(2,1)S(1)}, bf16[1,8,128,512]{3,2,1,0:T(8,128)(2,1)}, u32[]{:S(2)}) copy-start(bf16[1,8,128,512]{3,2,1,0:T(8,128)(2,1)} %param.6) | copy-start | bytes 3145732
  42.5 8.1 %copy-start.2 = (bf16[1,1,256,256]{3,2,1,0:T(8,128)(2,1)S(1)}, bf16[1,1,256,256]{3,2,1,0:T(8,128)(2,1)}, u32[]{:S(2)}) copy-start(bf16[1,1,256,256]{3,2,1,0:T(8,128)(2,1)} %param.8) | copy-start | bytes 393220
  49.5 1.1 copy-start.1
  50.5 183.1 %all-reduce.4.cloned.1.call-start = ((), (), s32[]{:S(2)}) async-start(), calls=%async_computation | async-start | bytes 3145728 | tf_op jit(solution)/shard_map/psum | solution.py:92
Sparse Core Ops, SparseCore 0:
  14.5 26.0 all-gather.4
  50.6 66.6 all-gather.6
Sparse Core Ops, SparseCore 1:
  56.8 176.7 all-reduce.3
